TPU v7x, 32 devices: a whole 2x2x4 slice. The times are simulated.
32 devices in a mesh: layout: 2 (over x), tile: 8 (over z, y), chan: 2 (over core).
Axes of the slice: x: 2, y: 2, z: 4, core: 2. Of those that a mesh axis runs over, the one named last changes fastest.
Arguments:
- sample_weight: float32 [32, 64, 256], P(('layout', 'tile', 'chan')), parts along dimension 0, may hold values from 0.25 to 4
- fraction_u: float32 [32, 64, 256], P(('layout', 'tile', 'chan')), parts along dimension 0, may hold values from 0 to 1
- fraction_v: float32 [32, 64, 256], P(('layout', 'tile', 'chan')), parts along dimension 0, may hold values from 0 to 1
- cell_code: int32 [32, 64, 256], P(('layout', 'tile', 'chan')), parts along dimension 0, may hold values from 260 to 3835, as said below
- tile_fill: int32 [32, 64, 64], P(('layout', 'tile', 'chan')), parts along dimension 0, may hold values from 0 to 4, as said below
Outputs:
- psf: float32 [8192, 4096], P(('layout', 'tile', 'chan')), parts along dimension 0
There are 2 independent parts, one for each index of `layout`. A program takes and returns all parts, laid end to end along the dimension named above; each array names one. Nothing has to cross between parts.
Inputs may be any that keep to these rules, and one draw needn't show every extreme that they name: `cell_code`: row offset and column offset each lie in 4 .. 59. `tile_fill`: some uv tile is full from every sender; tiles near the grid's centre hold more samples than outer ones.
All inputs are finite; a program needn't handle non-finite values.
Results may differ from a plain program's by a relative error of at most 0.0003.
Values sent between devices are 32-bit elements; how exact they have to be, the bound alone decides.
No kernel may reach another device: no remote copies, remote signals or barrier semaphores. Data moves between devices by JAX's collectives and lax.ppermute only.
A program may use at most 64 MiB of HBM per device.

v0:
```python
import math

import jax
import jax.numpy as jnp
from jax import lax
from jax.sharding import PartitionSpec as P

G = 4096
TILE = 64
HALF = 3
CAP = 4
NT = 64


HIGHEST = lax.Precision.HIGHEST


def taper(distance):
    scaled = distance / (HALF + 1.0)
    inner = 1.0 - scaled * scaled
    return jnp.where(inner > 0.0, inner * inner, 0.0 * inner)


def angles(left_count, right_count, period):
    product = (
        jnp.arange(left_count, dtype=jnp.int32)[:, None]
        * jnp.arange(right_count, dtype=jnp.int32)[None, :]
    )
    phase = (product % period).astype(jnp.float32) * (2.0 * math.pi / period)
    return (jnp.cos(phase), jnp.sin(phase))


def grid_row(weight_row, frac_row_u, frac_row_v, code_row, fill_row):
    sources = weight_row.shape[0]
    cell_pos = jnp.arange(TILE).astype(jnp.float32)
    slot_index = jnp.arange(CAP, dtype=jnp.int32)
    weight_row = weight_row.reshape(sources, NT, CAP)
    code_row = code_row.reshape(sources, NT, CAP)
    is_live = slot_index[None, None, :] < fill_row[:, :, None]
    live_weight = jnp.where(is_live, weight_row, 0.0)
    row_off = (code_row // TILE).astype(jnp.float32) + frac_row_u.reshape(sources, NT, CAP)
    col_off = (code_row % TILE).astype(jnp.float32) + frac_row_v.reshape(sources, NT, CAP)
    kernel_u = taper(cell_pos - row_off[..., None]) * live_weight[..., None]
    kernel_v = taper(cell_pos - col_off[..., None])
    tiles = jnp.einsum("sncu,sncv->unv", kernel_u, kernel_v, precision=HIGHEST)
    return tiles.reshape(TILE, G)


def row_pass(slab):
    slab_rows = slab.shape[0]
    blocks = slab.reshape(slab_rows, NT, TILE)
    cos_small, sin_small = angles(NT, NT, NT)
    first_re = jnp.einsum("rab,ak->rkb", blocks, cos_small, precision=HIGHEST)
    first_im = jnp.einsum("rab,ak->rkb", blocks, sin_small, precision=HIGHEST)
    cos_twist, sin_twist = angles(NT, TILE, G)
    turned_re = first_re * cos_twist - first_im * sin_twist
    turned_im = first_re * sin_twist + first_im * cos_twist
    cos_large, sin_large = angles(TILE, TILE, TILE)
    out_re = jnp.einsum("rkb,bj->rjk", turned_re, cos_large, precision=HIGHEST) - jnp.einsum(
        "rkb,bj->rjk", turned_im, sin_large, precision=HIGHEST
    )
    out_im = jnp.einsum("rkb,bj->rjk", turned_re, sin_large, precision=HIGHEST) + jnp.einsum(
        "rkb,bj->rjk", turned_im, cos_large, precision=HIGHEST
    )
    return (out_re.reshape(slab_rows, G), out_im.reshape(slab_rows, G))


def column_pass(part_re, part_im):
    col_count = part_re.shape[1]
    blocks_re = part_re.reshape(NT, TILE, col_count)
    blocks_im = part_im.reshape(NT, TILE, col_count)
    cos_small, sin_small = angles(NT, NT, NT)
    first_re = jnp.einsum("abc,ak->kbc", blocks_re, cos_small, precision=HIGHEST) - jnp.einsum(
        "abc,ak->kbc", blocks_im, sin_small, precision=HIGHEST
    )
    first_im = jnp.einsum("abc,ak->kbc", blocks_re, sin_small, precision=HIGHEST) + jnp.einsum(
        "abc,ak->kbc", blocks_im, cos_small, precision=HIGHEST
    )
    cos_twist, sin_twist = angles(NT, TILE, G)
    turned_re = first_re * cos_twist[:, :, None] - first_im * sin_twist[:, :, None]
    turned_im = first_re * sin_twist[:, :, None] + first_im * cos_twist[:, :, None]
    cos_large, sin_large = angles(TILE, TILE, TILE)
    real_part = jnp.einsum("kbc,bj->cjk", turned_re, cos_large, precision=HIGHEST) - jnp.einsum(
        "kbc,bj->cjk", turned_im, sin_large, precision=HIGHEST
    )
    return real_part.reshape(col_count, G)


def body(sample_weight, fraction_u, fraction_v, cell_code, tile_fill):
    landed_weight, landed_frac_u, landed_frac_v = (
        lax.all_to_all(sample_weight, "tile", split_axis=1, concat_axis=0, tiled=True),
        lax.all_to_all(fraction_u, "tile", split_axis=1, concat_axis=0, tiled=True),
        lax.all_to_all(fraction_v, "tile", split_axis=1, concat_axis=0, tiled=True),
    )
    landed_code, landed_fill = (
        lax.all_to_all(cell_code, "tile", split_axis=1, concat_axis=0, tiled=True),
        lax.all_to_all(tile_fill, "tile", split_axis=1, concat_axis=0, tiled=True),
    )
    own_rows = landed_weight.shape[1]
    row_slabs = []
    for local_row in range(own_rows):
        row_slabs.append(
            grid_row(
                landed_weight[:, local_row],
                landed_frac_u[:, local_row],
                landed_frac_v[:, local_row],
                landed_code[:, local_row],
                landed_fill[:, local_row],
            )
        )
    slab = jnp.concatenate(row_slabs, axis=0)
    tile_count = lax.axis_size("tile")
    chan_count = lax.axis_size("chan")
    shared = lax.psum_scatter(slab, "chan", scatter_dimension=0, tiled=True)
    spectrum_re, spectrum_im = row_pass(shared)
    column_re, column_im = (
        lax.all_to_all(spectrum_re, ("tile", "chan"), split_axis=1, concat_axis=0, tiled=True),
        lax.all_to_all(spectrum_im, ("tile", "chan"), split_axis=1, concat_axis=0, tiled=True),
    )
    norm_scale = 1.0 / math.sqrt(tile_count * chan_count * NT * NT * CAP)
    return column_pass(column_re, column_im) * norm_scale


def solution(mesh):
    return jax.shard_map(
        body,
        mesh=mesh,
        in_specs=(
            P(("layout", "tile", "chan"), None, None),
            P(("layout", "tile", "chan"), None, None),
            P(("layout", "tile", "chan"), None, None),
            P(("layout", "tile", "chan"), None, None),
            P(("layout", "tile", "chan"), None, None),
        ),
        out_specs=P(("layout", "tile", "chan"), None),
        check_vma=False,
    )
```

profile of v0, /device:TPU:13, one launch (start us, length us, event | category | flops | bytes accessed | tf_op | source)
XLA Modules:
  0.0 440.0 jit_solution(15600848524623938912)
XLA Ops:
  7.1 1.5 reduce
  9.3 5.7 %all-to-all-start.3 = ((s32[8,1,512]{2,1,0:T(1,128)}), s32[8,1,512]{2,1,0:T(1,128)S(1)}, u32[]{:S(2)}, u32[]{:S(2)}) async-start(s32[8,1,512]{2,1,0:T(1,128)} %reshape.720), calls=%async_computation.3 | async-start | bytes 32768 | tf_op jit(solution)/shard_map/all_to_all | solution.py:97
  15.0 1.5 copy.197
  16.5 1.5 copy.199
  18.1 1.5 copy.201
  19.6 1.5 copy.205
  21.1 5.4 %all-to-all-start = ((s32[1,64,256]{2,0,1:T(1,128)}), s32[1,64,256]{2,0,1:T(1,128)S(1)}, u32[]{:S(2)}, u32[]{:S(2)}) async-start(s32[1,64,256]{2,0,1:T(1,128)} %copy.197), calls=%async_computation | async-start | bytes 131072 | tf_op jit(solution)/shard_map/all_to_all | solution.py:96
  32.3 5.4 %all-to-all-start.1 = ((f32[1,64,256]{2,0,1:T(1,128)}), f32[1,64,256]{2,0,1:T(1,128)S(1)}, u32[]{:S(2)}, u32[]{:S(2)}) async-start(f32[1,64,256]{2,0,1:T(1,128)} %copy.199), calls=%async_computation.1 | async-start | bytes 131072 | tf_op jit(solution)/shard_map/all_to_all | solution.py:93
  37.9 3.7 all-to-all-done.1
  41.6 5.1 %all-to-all-start.2 = ((f32[1,64,256]{2,0,1:T(1,128)}), f32[1,64,256]{2,0,1:T(1,128)S(1)}, u32[]{:S(2)}, u32[]{:S(2)}) async-start(f32[1,64,256]{2,0,1:T(1,128)} %copy.201), calls=%async_computation.2 | async-start | bytes 131072 | tf_op jit(solution)/shard_map/all_to_all | solution.py:92
  47.0 3.6 all-to-all-done.2
  50.6 5.3 %all-to-all-start.4 = ((f32[1,64,256]{2,0,1:T(1,128)}), f32[1,64,256]{2,0,1:T(1,128)S(1)}, u32[]{:S(2)}, u32[]{:S(2)}) async-start(f32[1,64,256]{2,0,1:T(1,128)} %copy.205), calls=%async_computation.4 | async-start | bytes 131072 | tf_op jit(solution)/shard_map/all_to_all | solution.py:91
  56.0 3.6 all-to-all-done.4
  60.6 0.8 copy.218
  68.5 0.8 copy.231
  72.8 0.8 copy.241
  75.1 4.3 fusion.86
  79.8 5.8 %fusion.76 = f32[64,64,64,1]{2,1,3,0:T(8,128)} fusion(f32[8,64,4]{0,2,1:T(4,128)S(1)} %get-tuple-element.68, f32[8,64,4]{0,2,1:T(4,128)S(1)} %get-tuple-element.18, f32[8,64,4]{0,2,1:T(4,128)S(1)} %get-tuple-element.17, f32[64]{0:T(128)S(1)} %iota_convert_fusion), kind=kOutput, calls=%fused_computation.81 | convolution fusion | flops 102891520 | bytes 1073408 | tf_op jit(solution)/shard_map/sncu,sncv->unv/dot_general | solution.py:45
  86.0 5.6 %fusion.66 = f32[64,64,64,1]{2,1,3,0:T(8,128)} fusion(f32[8,64,4]{0,2,1:T(4,128)S(1)} %get-tuple-element.69, f32[8,64,4]{0,2,1:T(4,128)S(1)} %get-tuple-element.16, f32[8,64,4]{0,2,1:T(4,128)S(1)} %get-tuple-element.15, f32[64]{0:T(128)S(1)} %iota_convert_fusion), kind=kOutput, calls=%fused_computation.69 | convolution fusion | flops 102891520 | bytes 1073408 | tf_op jit(solution)/shard_map/sncu,sncv->unv/dot_general | solution.py:45
  92.0 5.5 %fusion.56 = f32[64,64,64,1]{2,1,3,0:T(8,128)} fusion(f32[8,64,4]{0,2,1:T(4,128)S(1)} %get-tuple-element.70, f32[8,64,4]{0,2,1:T(4,128)S(1)} %get-tuple-element.14, f32[8,64,4]{0,2,1:T(4,128)S(1)} %get-tuple-element.13, f32[64]{0:T(128)S(1)} %iota_convert_fusion), kind=kOutput, calls=%fused_computation.57 | convolution fusion | flops 102891520 | bytes 1073408 | tf_op jit(solution)/shard_map/sncu,sncv->unv/dot_general | solution.py:45
  97.8 5.5 %fusion.46 = f32[64,64,64,1]{2,1,3,0:T(8,128)} fusion(f32[8,64,4]{0,2,1:T(4,128)S(1)} %get-tuple-element.71, f32[8,64,4]{0,2,1:T(4,128)S(1)} %get-tuple-element.12, f32[8,64,4]{0,2,1:T(4,128)S(1)} %get-tuple-element.11, f32[64]{0:T(128)S(1)} %iota_convert_fusion), kind=kOutput, calls=%fused_computation.45 | convolution fusion | flops 102891520 | bytes 1073408 | tf_op jit(solution)/shard_map/sncu,sncv->unv/dot_general | solution.py:45
  103.7 6.1 %fusion.36 = f32[64,64,64,1]{2,1,3,0:T(8,128)} fusion(f32[8,64,4]{0,2,1:T(4,128)S(1)} %get-tuple-element.72, f32[8,64,4]{0,2,1:T(4,128)S(1)} %get-tuple-element.10, f32[8,64,4]{0,2,1:T(4,128)S(1)} %get-tuple-element.9, f32[64]{0:T(128)S(1)} %iota_convert_fusion), kind=kOutput, calls=%fused_computation.33 | convolution fusion | flops 102891520 | bytes 1073408 | tf_op jit(solution)/shard_map/sncu,sncv->unv/dot_general | solution.py:45
  110.0 5.5 %fusion.96 = f32[64,64,64,1]{2,1,3,0:T(8,128)} fusion(f32[8,64,4]{0,2,1:T(4,128)S(1)} %get-tuple-element.66, f32[8,64,4]{0,2,1:T(4,128)S(1)} %get-tuple-element.22, f32[8,64,4]{0,2,1:T(4,128)S(1)} %get-tuple-element.21, f32[64]{0:T(128)S(1)} %iota_convert_fusion), kind=kOutput, calls=%fused_computation.105 | convolution fusion | flops 102891520 | bytes 1073408 | tf_op jit(solution)/shard_map/sncu,sncv->unv/dot_general | solution.py:45
  115.9 5.5 %fusion.106 = f32[64,64,64,1]{2,1,3,0:T(8,128)} fusion(f32[8,64,4]{0,2,1:T(4,128)S(1)} %get-tuple-element.65, f32[8,64,4]{0,2,1:T(4,128)S(1)} %get-tuple-element.24, f32[8,64,4]{0,2,1:T(4,128)S(1)} %get-tuple-element.23, f32[64]{0:T(128)S(1)} %iota_convert_fusion), kind=kOutput, calls=%fused_computation.117 | convolution fusion | flops 102891520 | bytes 1073408 | tf_op jit(solution)/shard_map/sncu,sncv->unv/dot_general | solution.py:45
  121.4 14.2 %concatenate.3 = f32[512,4096]{0,1:T(8,128)} concatenate(f32[64,4096]{0,1:T(8,128)} %bitcast.168, f32[64,4096]{0,1:T(8,128)} %bitcast.167, f32[64,4096]{0,1:T(8,128)S(1)} %bitcast.161, f32[64,4096]{0,1:T(8,128)} %bitcast.162, f32[64,4096]{0,1:T(8,128)} %bitcast.163, f32[64,4096]{0,1:T(8,128)} %bitcast.164, f32[64,4096]{0,1:T(8,128)} %bitcast.165, f32[64,4096]{0,1:T(8,128)} %bitcast.166), dimensions={0} | concatenate | bytes 16777216 | tf_op jit(solution)/shard_map/concatenate | solution.py:111
  135.8 21.0 %reduce-scatter.2.cloned.1.call-done = f32[256,4096]{0,1:T(8,128)} async-done(((f32[512,4096]{0,1:T(8,128)}), f32[256,4096]{0,1:T(8,128)}) %reduce-scatter.2.cloned.1.call-update) | async-done | bytes 4194320 | tf_op jit(solution)/shard_map/reduce_scatter | solution.py:114
  156.8 8.7 %fusion.20 = f32[64,256,64]{1,0,2:T(8,128)S(1)} fusion(f32[256,64,64]{0,2,1:T(8,128)} %bitcast.159), kind=kOutput, calls=%fused_computation.27 | convolution fusion | flops 805363712 | bytes 8388608 | tf_op jit(solution)/shard_map/rab,ak->rkb/dot_general | solution.py:54
  165.5 7.8 %subtract_bitcast_fusion.1 = (f32[256,64,64]{0,1,2:T(8,128)S(1)}, f32[256,64,64]{0,1,2:T(8,128)S(1)}) fusion(f32[64,256,64]{1,0,2:T(8,128)S(1)} %fusion.20, f32[64,64]{0,1:T(8,128)S(1)} %get-tuple-element.73, f32[64,64]{0,1:T(8,128)S(1)} %get-tuple-element.74, f32[256,64,64]{0,2,1:T(8,128)S(1)} %bitcast.160), kind=kOutput, calls=%fused_computation.10 | convolution fusion | flops 811655168 | bytes 16809984 | tf_op jit(solution)/shard_map/rab,ak->rkb/dot_general | solution.py:53
  173.3 6.3 %fusion.12 = f32[64,256,64]{1,0,2:T(8,128)S(1)} fusion(f32[256,64,64]{0,1,2:T(8,128)S(1)} %get-tuple-element.8), kind=kOutput, calls=%fused_computation.19 | convolution fusion | flops 805363712 | bytes 8388608 | tf_op jit(solution)/shard_map/rkb,bj->rjk/dot_general | solution.py:62
  179.6 6.4 %add_bitcast_fusion = f32[256,64,64]{0,1,2:T(8,128)S(1)} fusion(f32[64,256,64]{1,0,2:T(8,128)S(1)} %fusion.12, f32[256,64,64]{0,1,2:T(8,128)S(1)} %get-tuple-element.7), kind=kOutput, calls=%fused_computation.7 | convolution fusion | flops 806412288 | bytes 12582912 | tf_op jit(solution)/shard_map/rkb,bj->rjk/dot_general | solution.py:62
  186.0 4.4 %copy.251 = f32[256,64,64]{0,2,1:T(8,128)} copy(f32[256,64,64]{0,1,2:T(8,128)S(1)} %add_bitcast_fusion) | data formatting | bytes 8388608 | tf_op jit(solution)/shard_map/add | solution.py:62
  190.5 6.6 %all-to-all-start.6 = ((f32[256,16,256]{0,2,1:T(8,128)}), f32[256,16,256]{0,2,1:T(8,128)}, u32[]{:S(2)}, u32[]{:S(2)}) async-start(f32[256,16,256]{0,2,1:T(8,128)} %bitcast.157), calls=%async_computation.7 | async-start | bytes 8388608 | tf_op jit(solution)/shard_map/all_to_all | solution.py:118
  197.1 8.6 %fusion.14 = f32[64,256,64]{1,0,2:T(8,128)S(1)} fusion(f32[256,64,64]{0,1,2:T(8,128)} %copy-done.4), kind=kOutput, calls=%fused_computation.21 | convolution fusion | flops 805363712 | bytes 8388608 | tf_op jit(solution)/shard_map/rkb,bj->rjk/dot_general | solution.py:59
  205.7 6.0 %subtract_bitcast_fusion = f32[256,64,64]{0,1,2:T(8,128)S(1)} fusion(f32[64,256,64]{1,0,2:T(8,128)S(1)} %fusion.14, f32[256,64,64]{0,1,2:T(8,128)S(1)} %copy-done.2), kind=kOutput, calls=%fused_computation.8 | convolution fusion | flops 806412288 | bytes 12582912 | tf_op jit(solution)/shard_map/rkb,bj->rjk/dot_general | solution.py:59
  211.7 4.5 %copy.246 = f32[256,64,64]{0,2,1:T(8,128)} copy(f32[256,64,64]{0,1,2:T(8,128)S(1)} %subtract_bitcast_fusion) | data formatting | bytes 8388608 | tf_op jit(solution)/shard_map/sub | solution.py:59
  216.2 73.2 %all-to-all-done.6 = f32[256,16,256]{0,2,1:T(8,128)} async-done(((f32[256,16,256]{0,2,1:T(8,128)}), f32[256,16,256]{0,2,1:T(8,128)}, u32[]{:S(2)}, u32[]{:S(2)}) %all-to-all-start.6) | async-done | bytes 4194336 | tf_op jit(solution)/shard_map/all_to_all | solution.py:118
  289.4 4.8 %all-to-all-start.5 = ((f32[256,16,256]{0,2,1:T(8,128)}), f32[256,16,256]{0,2,1:T(8,128)}, u32[]{:S(2)}, u32[]{:S(2)}) async-start(f32[256,16,256]{0,2,1:T(8,128)} %bitcast.156), calls=%async_computation.6 | async-start | bytes 8388608 | tf_op jit(solution)/shard_map/all_to_all | solution.py:117
  294.1 5.3 %copy.252 = f32[16,256,256]{2,1,0:T(8,128)} copy(f32[16,256,256]{1,2,0:T(8,128)} %bitcast.85) | data formatting | bytes 8388608 | tf_op jit(solution)/shard_map/all_to_all | solution.py:118
  299.5 10.3 %fusion.6 = f32[64,64,256]{2,0,1:T(8,128)} fusion(f32[64,64,256]{2,1,0:T(8,128)} %bitcast.154), kind=kOutput, calls=%fused_computation.13 | convolution fusion | flops 805363712 | bytes 8388608 | tf_op jit(solution)/shard_map/abc,ak->kbc/dot_general | solution.py:73
  309.8 7.0 %fusion.4 = f32[64,64,256]{2,0,1:T(8,128)} fusion(f32[64,64,256]{2,1,0:T(8,128)S(1)} %bitcast.155), kind=kOutput, calls=%fused_computation.11 | convolution fusion | flops 805363712 | bytes 8388608 | tf_op jit(solution)/shard_map/abc,ak->kbc/dot_general | solution.py:76
  316.8 69.8 %all-to-all-done.5 = f32[256,16,256]{0,2,1:T(8,128)} async-done(((f32[256,16,256]{0,2,1:T(8,128)}), f32[256,16,256]{0,2,1:T(8,128)}, u32[]{:S(2)}, u32[]{:S(2)}) %all-to-all-start.5) | async-done | bytes 4194336 | tf_op jit(solution)/shard_map/all_to_all | solution.py:117
  386.6 5.5 %copy.247 = f32[16,256,256]{2,1,0:T(8,128)} copy(f32[16,256,256]{1,2,0:T(8,128)} %bitcast.81) | data formatting | bytes 8388608 | tf_op jit(solution)/shard_map/all_to_all | solution.py:117
  392.1 10.0 %fusion.28 = f32[64,64,256]{2,0,1:T(8,128)S(1)} fusion(f32[64,64,256]{2,0,1:T(8,128)} %fusion.6, f32[64,64,256]{2,1,0:T(8,128)} %bitcast.152), kind=kOutput, calls=%fused_computation.31 | convolution fusion | flops 806412288 | bytes 12582912 | tf_op jit(solution)/shard_map/abc,ak->kbc/dot_general | solution.py:73
  402.1 8.4 %multiply_subtract_fusion = (f32[64,64,256]{2,0,1:T(8,128)S(1)}, f32[64,64,256]{2,0,1:T(8,128)S(1)}) fusion(f32[64,64,256]{2,0,1:T(8,128)S(1)} %fusion.28, f32[64,64]{0,1:T(8,128)S(1)} %get-tuple-element.73, f32[64,64]{0,1:T(8,128)S(1)} %get-tuple-element.74, f32[64,64,256]{2,0,1:T(8,128)S(1)} %copy-done.5, f32[64,64,256]{2,1,0:T(8,128)S(1)} %bitcast.153), kind=kOutput, calls=%fused_computation.6 | convolution fusion | flops 812703744 | bytes 21004288 | tf_op jit(solution)/shard_map/abc,ak->kbc/dot_general | solution.py:76
  410.6 6.0 %fusion = f32[64,64,256]{2,0,1:T(8,128)S(1)} fusion(f32[64,64,256]{2,0,1:T(8,128)S(1)} %get-tuple-element.6), kind=kOutput, calls=%fused_computation | convolution fusion | flops 805363712 | bytes 8388608 | tf_op jit(solution)/shard_map/kbc,bj->cjk/dot_general | solution.py:83
  416.6 6.4 %multiply_bitcast_fusion = f32[256,64,64]{0,1,2:T(8,128)S(1)} fusion(f32[64,64,256]{2,0,1:T(8,128)S(1)} %fusion, f32[64,64,256]{2,0,1:T(8,128)S(1)} %get-tuple-element.5), kind=kOutput, calls=%fused_computation.4 | convolution fusion | flops 807460864 | bytes 12582912 | tf_op jit(solution)/shard_map/kbc,bj->cjk/dot_general | solution.py:83
  423.0 4.4 %copy.258 = f32[256,64,64]{0,2,1:T(8,128)} copy(f32[256,64,64]{0,1,2:T(8,128)S(1)} %multiply_bitcast_fusion) | data formatting | bytes 8388608 | tf_op jit(solution)/shard_map/mul | solution.py:121
  427.4 5.6 %copy.259 = f32[256,4096]{1,0:T(8,128)} copy(f32[256,4096]{0,1:T(8,128)} %bitcast.158) | data formatting | bytes 8388608 | tf_op jit(solution)/shard_map/mul | solution.py:121
  (126 shorter events, 22.7 us)
Async XLA Ops:
  9.3 11.8 %all-to-all-start.3 = ((s32[8,1,512]{2,1,0:T(1,128)}), s32[8,1,512]{2,1,0:T(1,128)S(1)}, u32[]{:S(2)}, u32[]{:S(2)}) async-start(s32[8,1,512]{2,1,0:T(1,128)} %reshape.720), calls=%async_computation.3 | async-start | bytes 32768 | tf_op jit(solution)/shard_map/all_to_all | solution.py:97
  21.1 11.2 %all-to-all-start = ((s32[1,64,256]{2,0,1:T(1,128)}), s32[1,64,256]{2,0,1:T(1,128)S(1)}, u32[]{:S(2)}, u32[]{:S(2)}) async-start(s32[1,64,256]{2,0,1:T(1,128)} %copy.197), calls=%async_computation | async-start | bytes 131072 | tf_op jit(solution)/shard_map/all_to_all | solution.py:96
  32.3 9.3 %all-to-all-start.1 = ((f32[1,64,256]{2,0,1:T(1,128)}), f32[1,64,256]{2,0,1:T(1,128)S(1)}, u32[]{:S(2)}, u32[]{:S(2)}) async-start(f32[1,64,256]{2,0,1:T(1,128)} %copy.199), calls=%async_computation.1 | async-start | bytes 131072 | tf_op jit(solution)/shard_map/all_to_all | solution.py:93
  41.6 8.9 %all-to-all-start.2 = ((f32[1,64,256]{2,0,1:T(1,128)}), f32[1,64,256]{2,0,1:T(1,128)S(1)}, u32[]{:S(2)}, u32[]{:S(2)}) async-start(f32[1,64,256]{2,0,1:T(1,128)} %copy.201), calls=%async_computation.2 | async-start | bytes 131072 | tf_op jit(solution)/shard_map/all_to_all | solution.py:92
  50.6 9.0 %all-to-all-start.4 = ((f32[1,64,256]{2,0,1:T(1,128)}), f32[1,64,256]{2,0,1:T(1,128)S(1)}, u32[]{:S(2)}, u32[]{:S(2)}) async-start(f32[1,64,256]{2,0,1:T(1,128)} %copy.205), calls=%async_computation.4 | async-start | bytes 131072 | tf_op jit(solution)/shard_map/all_to_all | solution.py:91
  55.8 100.9 %reduce-scatter.2.cloned.1.call-start = ((), (), s32[]{:S(2)}) async-start(), calls=%async_computation.8 | async-start | bytes 12582912 | tf_op jit(solution)/shard_map/reduce_scatter | solution.py:114
  75.0 4.4 copy-start.20
  75.0 4.4 copy-start.21
  75.1 4.4 copy-start.22
  75.1 4.4 copy-start.23
  75.1 4.4 copy-start.30
  79.8 5.9 %copy-start.16 = (s32[8,1,256]{0,2,1:T(8,128)S(1)}, s32[8,1,256]{0,2,1:T(8,128)}, u32[]{:S(2)}) copy-start(s32[8,1,256]{0,2,1:T(8,128)} %copy.222) | copy-start | bytes 24580
  79.8 5.9 %copy-start.17 = (f32[8,1,256]{0,2,1:T(8,128)S(1)}, f32[8,1,256]{0,2,1:T(8,128)}, u32[]{:S(2)}) copy-start(f32[8,1,256]{0,2,1:T(8,128)} %copy.223) | copy-start | bytes 24580
  79.8 5.9 %copy-start.18 = (f32[8,1,256]{0,2,1:T(8,128)S(1)}, f32[8,1,256]{0,2,1:T(8,128)}, u32[]{:S(2)}) copy-start(f32[8,1,256]{0,2,1:T(8,128)} %copy.224) | copy-start | bytes 24580
  79.8 5.8 %copy-start.19 = (f32[8,1,256]{0,2,1:T(8,128)S(1)}, f32[8,1,256]{0,2,1:T(8,128)}, u32[]{:S(2)}) copy-start(f32[8,1,256]{0,2,1:T(8,128)} %copy.226) | copy-start | bytes 24580
  79.8 5.8 %copy-start.29 = (s32[8,1,64]{0,2,1:T(8,128)S(1)}, s32[8,1,64]{0,2,1:T(8,128)}, u32[]{:S(2)}) copy-start(s32[8,1,64]{0,2,1:T(8,128)} %copy.276) | copy-start | bytes 6148
  85.9 5.7 %copy-start.12 = (s32[8,1,256]{0,2,1:T(8,128)S(1)}, s32[8,1,256]{0,2,1:T(8,128)}, u32[]{:S(2)}) copy-start(s32[8,1,256]{0,2,1:T(8,128)} %copy.227) | copy-start | bytes 24580
  85.9 5.7 %copy-start.13 = (f32[8,1,256]{0,2,1:T(8,128)S(1)}, f32[8,1,256]{0,2,1:T(8,128)}, u32[]{:S(2)}) copy-start(f32[8,1,256]{0,2,1:T(8,128)} %copy.228) | copy-start | bytes 24580
  86.0 5.7 %copy-start.14 = (f32[8,1,256]{0,2,1:T(8,128)S(1)}, f32[8,1,256]{0,2,1:T(8,128)}, u32[]{:S(2)}) copy-start(f32[8,1,256]{0,2,1:T(8,128)} %copy.229) | copy-start | bytes 24580
  86.0 5.6 %copy-start.15 = (f32[8,1,256]{0,2,1:T(8,128)S(1)}, f32[8,1,256]{0,2,1:T(8,128)}, u32[]{:S(2)}) copy-start(f32[8,1,256]{0,2,1:T(8,128)} %copy.231) | copy-start | bytes 24580
  86.0 5.6 %copy-start.28 = (s32[8,1,64]{0,2,1:T(8,128)S(1)}, s32[8,1,64]{0,2,1:T(8,128)}, u32[]{:S(2)}) copy-start(s32[8,1,64]{0,2,1:T(8,128)} %copy.277) | copy-start | bytes 6148
  91.9 5.6 %copy-start.8 = (s32[8,1,256]{0,2,1:T(8,128)S(1)}, s32[8,1,256]{0,2,1:T(8,128)}, u32[]{:S(2)}) copy-start(s32[8,1,256]{0,2,1:T(8,128)} %copy.232) | copy-start | bytes 24580
  91.9 5.6 %copy-start.9 = (f32[8,1,256]{0,2,1:T(8,128)S(1)}, f32[8,1,256]{0,2,1:T(8,128)}, u32[]{:S(2)}) copy-start(f32[8,1,256]{0,2,1:T(8,128)} %copy.233) | copy-start | bytes 24580
  91.9 5.6 %copy-start.10 = (f32[8,1,256]{0,2,1:T(8,128)S(1)}, f32[8,1,256]{0,2,1:T(8,128)}, u32[]{:S(2)}) copy-start(f32[8,1,256]{0,2,1:T(8,128)} %copy.234) | copy-start | bytes 24580
  91.9 5.6 %copy-start.11 = (f32[8,1,256]{0,2,1:T(8,128)S(1)}, f32[8,1,256]{0,2,1:T(8,128)}, u32[]{:S(2)}) copy-start(f32[8,1,256]{0,2,1:T(8,128)} %copy.236) | copy-start | bytes 24580
  92.0 5.6 %copy-start.27 = (s32[8,1,64]{0,2,1:T(8,128)S(1)}, s32[8,1,64]{0,2,1:T(8,128)}, u32[]{:S(2)}) copy-start(s32[8,1,64]{0,2,1:T(8,128)} %copy.278) | copy-start | bytes 6148
  97.8 5.6 %copy-start.7 = (f32[8,1,256]{0,2,1:T(8,128)S(1)}, f32[8,1,256]{0,2,1:T(8,128)}, u32[]{:S(2)}) copy-start(f32[8,1,256]{0,2,1:T(8,128)} %copy.241) | copy-start | bytes 24580
  97.8 5.6 %copy-start.26 = (s32[8,1,64]{0,2,1:T(8,128)S(1)}, s32[8,1,64]{0,2,1:T(8,128)}, u32[]{:S(2)}) copy-start(s32[8,1,64]{0,2,1:T(8,128)} %copy.279) | copy-start | bytes 6148
  103.7 6.1 %copy-start.25 = (s32[8,1,64]{0,2,1:T(8,128)S(1)}, s32[8,1,64]{0,2,1:T(8,128)}, u32[]{:S(2)}) copy-start(s32[8,1,64]{0,2,1:T(8,128)} %copy.273) | copy-start | bytes 6148
  110.0 5.6 %copy-start.24 = (s32[8,1,64]{0,2,1:T(8,128)S(1)}, s32[8,1,64]{0,2,1:T(8,128)}, u32[]{:S(2)}) copy-start(s32[8,1,64]{0,2,1:T(8,128)} %copy.272) | copy-start | bytes 6148
  156.8 8.8 %copy-start.6 = (f32[256,4096]{0,1:T(8,128)S(1)}, f32[256,4096]{0,1:T(8,128)}, u32[]{:S(2)}) copy-start(f32[256,4096]{0,1:T(8,128)} %reduce-scatter.2.cloned.1.call-done) | copy-start | bytes 12582916
  173.3 6.3 %copy-start.4 = (f32[256,64,64]{0,1,2:T(8,128)}, f32[256,64,64]{0,1,2:T(8,128)S(1)}, u32[]{:S(2)}) copy-start(f32[256,64,64]{0,1,2:T(8,128)S(1)} %get-tuple-element.8) | copy-start | bytes 12582916
  173.3 6.3 %copy-start.1 = (f32[256,64,64]{0,1,2:T(8,128)}, f32[256,64,64]{0,1,2:T(8,128)S(1)}, u32[]{:S(2)}) copy-start(f32[256,64,64]{0,1,2:T(8,128)S(1)} %get-tuple-element.7) | copy-start | bytes 12582916
  190.5 98.9 %all-to-all-start.6 = ((f32[256,16,256]{0,2,1:T(8,128)}), f32[256,16,256]{0,2,1:T(8,128)}, u32[]{:S(2)}, u32[]{:S(2)}) async-start(f32[256,16,256]{0,2,1:T(8,128)} %bitcast.157), calls=%async_computation.7 | async-start | bytes 8388608 | tf_op jit(solution)/shard_map/all_to_all | solution.py:118
  197.1 8.6 %copy-start.2 = (f32[256,64,64]{0,1,2:T(8,128)S(1)}, f32[256,64,64]{0,1,2:T(8,128)}, u32[]{:S(2)}) copy-start(f32[256,64,64]{0,1,2:T(8,128)} %copy-done.1) | copy-start | bytes 12582916
  289.4 97.2 %all-to-all-start.5 = ((f32[256,16,256]{0,2,1:T(8,128)}), f32[256,16,256]{0,2,1:T(8,128)}, u32[]{:S(2)}, u32[]{:S(2)}) async-start(f32[256,16,256]{0,2,1:T(8,128)} %bitcast.156), calls=%async_computation.6 | async-start | bytes 8388608 | tf_op jit(solution)/shard_map/all_to_all | solution.py:117
  299.5 10.3 %copy-start.3 = (f32[16,256,256]{2,1,0:T(8,128)S(1)}, f32[16,256,256]{2,1,0:T(8,128)}, u32[]{:S(2)}) copy-start(f32[16,256,256]{2,1,0:T(8,128)} %copy.252) | copy-start | bytes 12582916
  392.1 10.0 %copy-start = (f32[16,256,256]{2,1,0:T(8,128)S(1)}, f32[16,256,256]{2,1,0:T(8,128)}, u32[]{:S(2)}) copy-start(f32[16,256,256]{2,1,0:T(8,128)} %copy.247) | copy-start | bytes 12582916
  392.1 10.0 %copy-start.5 = (f32[64,64,256]{2,0,1:T(8,128)S(1)}, f32[64,64,256]{2,0,1:T(8,128)}, u32[]{:S(2)}) copy-start(f32[64,64,256]{2,0,1:T(8,128)} %fusion.4) | copy-start | bytes 12582916
Sparse Core Ops, SparseCore 0:
  135.7 20.9 reduce-scatter.1
where the time goes:
time: 448 us; the launch traced here: 440 us
  waiting for transfers between devices  175 us (39%)
  matrix products  136 us (30%)
  local copies, waits for them, and re-layouts  72.1 us (16%)
  starting transfers between devices  38.3 us (9%)
  between operations  14.3 us (3%)
  other arithmetic  4.63 us (1%)
    all_to_all x1, waiting for transfers between devices, body(): lax.all_to_all(spectrum_im, ('tile', 'chan'), split_axis=1, concat_axis=0...  73.2 us
    all_to_all x1, waiting for transfers between devices, body(): lax.all_to_all(spectrum_re, ('tile', 'chan'), split_axis=1, concat_axis=0...  69.8 us
    dot_general x8, matrix products, grid_row(): tiles = jnp.einsum('sncu,sncv->unv', kernel_u, kernel_v, precision=HIGHEST)  44 us
    reduce_scatter x1, waiting for transfers between devices, body(): shared = lax.psum_scatter(slab, 'chan', scatter_dimension=0, tiled=True)  21 us
    concatenate x1, local copies, waits for them, and re-layouts, body(): slab = jnp.concatenate(row_slabs, axis=0)  14.2 us
    unnamed x81, local copies, waits for them, and re-layouts  12.5 us
    dot_general x1, matrix products, column_pass(): jnp.einsum('abc,ak->kbc', blocks_im, sin_small, precision=HIGHEST)  10.3 us
    mul x2, local copies, waits for them, and re-layouts, body(): return column_pass(column_re, column_im) * norm_scale  10 us
  transfers between devices with their start and end apart: 8, of which 6 were waited for; matrix products, arithmetic and copies ran while one was open for 12% of the time, Pallas kernels for 0%

commit v1 on v0

--- a/solution.py
+++ b/solution.py
@@ -2,8 +2,11 @@
 
 import jax
 import jax.numpy as jnp
+import numpy as np
 from jax import lax
-from jax.sharding import PartitionSpec as P
+from jax.experimental import pallas as pl
+from jax.experimental.pallas import tpu as pltpu
+from jax.sharding import Mesh, PartitionSpec as P
 
 G = 4096
 TILE = 64
@@ -86,7 +89,7 @@
     return real_part.reshape(col_count, G)
 
 
-def body(sample_weight, fraction_u, fraction_v, cell_code, tile_fill):
+def general_body(sample_weight, fraction_u, fraction_v, cell_code, tile_fill):
     landed_weight, landed_frac_u, landed_frac_v = (
         lax.all_to_all(sample_weight, "tile", split_axis=1, concat_axis=0, tiled=True),
         lax.all_to_all(fraction_u, "tile", split_axis=1, concat_axis=0, tiled=True),
@@ -121,17 +124,340 @@
     return column_pass(column_re, column_im) * norm_scale
 
 
+HALVES = 2
+LANES = 2 * TILE
+COARSE = G // LANES
+SLABS = NT // 4
+HERM = COARSE // 2 + 1
+BF16 = jnp.bfloat16
+F32 = jnp.float32
+
+
+def split(value):
+    high = value.astype(BF16)
+    return high, (value - high.astype(F32)).astype(BF16)
+
+
+def split_constant(value):
+    high = value.astype(np.float32).astype(BF16)
+    low = (value - high.astype(np.float64)).astype(np.float32).astype(BF16)
+    return high, low
+
+
+def exact_pieces(value):
+    high, rest = value.astype(BF16), None
+    rest = value - high.astype(F32)
+    middle = rest.astype(BF16)
+    return high, middle, (rest - middle.astype(F32)).astype(BF16)
+
+
+def times(value, turn):
+    real, imag = value
+    turn = turn % 1.0
+    if turn == 0.0:
+        return value
+    if turn == 0.25:
+        return (None if imag is None else -imag, real)
+    if turn == 0.5:
+        return (-real, None if imag is None else -imag)
+    c, s = math.cos(2 * math.pi * turn), math.sin(2 * math.pi * turn)
+    if imag is None:
+        return (real * c, real * s)
+    if turn == 0.125:
+        return ((real - imag) * c, (real + imag) * c)
+    if turn == 0.375:
+        return ((real + imag) * c, (real - imag) * s)
+    return (real * c - imag * s, real * s + imag * c)
+
+
+def plus(x, y):
+    if x is None:
+        return y
+    return x if y is None else x + y
+
+
+def minus(x, y):
+    if y is None:
+        return x
+    return -y if x is None else x - y
+
+
+def real_transform(values):
+    n = len(values)
+    if n == 1:
+        return [(values[0], None)]
+    if n == 2:
+        return [(values[0] + values[1], None), (values[0] - values[1], None)]
+    even, odd = real_transform(values[0::2]), real_transform(values[1::2])
+    out = [None] * (n // 2 + 1)
+    for k in range(n // 4 + 1):
+        e, t = even[k], times(odd[k], k / n)
+        out[k] = (plus(e[0], t[0]), plus(e[1], t[1]))
+        if n // 2 - k != k:
+            out[n // 2 - k] = (minus(e[0], t[0]), minus(t[1], e[1]))
+    return out
+
+
+def complex_transform(values):
+    n = len(values)
+    if n == 1:
+        return values
+    even, odd = complex_transform(values[0::2]), complex_transform(values[1::2])
+    out = [None] * n
+    for k in range(n // 2):
+        e, t = even[k], times(odd[k], k / n)
+        out[k] = (plus(e[0], t[0]), plus(e[1], t[1]))
+        out[k + n // 2] = (minus(e[0], t[0]), minus(e[1], t[1]))
+    return out
+
+
+def pack_kernel(weight_ref, frac_u_ref, frac_v_ref, code_ref, fill_ref, out_ref, stage_ref):
+    wide = NT * CAP
+    row = lax.broadcasted_iota(jnp.int32, (NT, wide), 0)
+    lane = lax.broadcasted_iota(jnp.int32, (NT, wide), 1)
+    spread = jnp.where(lane // CAP == row, 1.0, 0.0).astype(BF16)
+    filled = jnp.dot(fill_ref[0].astype(F32).astype(BF16), spread, preferred_element_type=F32)
+    live = jnp.where((lane % CAP).astype(F32) < filled, weight_ref[0], 0.0)
+    code = code_ref[0]
+    place_u = (code // TILE).astype(F32) + frac_u_ref[0]
+    place_v = (code % TILE).astype(F32) + frac_v_ref[0]
+    folded = row >= NT // 2
+    place_u = jnp.where(folded, TILE - place_u, place_u)
+    place_v = jnp.where(folded, TILE - place_v, place_v)
+    for arr, value in enumerate((live, place_u, place_v)):
+        for part in range(2):
+            stage_ref[2 * arr + part] = value[:, part * LANES : (part + 1) * LANES]
+    kappa = lax.broadcasted_iota(jnp.int32, (2 * wide, CAP * LANES), 0)
+    target = lax.broadcasted_iota(jnp.int32, (2 * wide, CAP * LANES), 1)
+    parity, column, slot = kappa // wide, (kappa % wide) // CAP, kappa % CAP
+    place = parity * NT + column
+    low = jnp.where(target == slot * LANES + place, 1.0, 0.0).astype(BF16)
+    high = jnp.where(target == slot * LANES + (LANES - 1 - place), 1.0, 0.0).astype(BF16)
+    pairs = NT // 2
+    rows = [
+        jnp.concatenate(
+            [stage_ref[2 * arr + part, pl.ds(parity, pairs, stride=2), :] for parity in range(2) for part in range(2)],
+            axis=1,
+        )
+        for arr in range(3)
+    ]
+    halves = pairs // 2
+    for fold, permute in enumerate((low, high)):
+        chosen = jnp.concatenate([value[fold * halves : (fold + 1) * halves] for value in rows], axis=0)
+        moved = sum(jnp.dot(piece, permute, preferred_element_type=F32) for piece in exact_pieces(chosen))
+        for arr in range(3):
+            for slot in range(CAP):
+                block = moved[arr * halves : (arr + 1) * halves, slot * LANES : (slot + 1) * LANES]
+                at = arr * 2 * CAP + fold * CAP + slot
+                for half in range(HALVES):
+                    if fold == 0:
+                        out_ref[half, pl.ds(at, halves, stride=6 * CAP), :] = block
+                    else:
+                        for slab in range(halves):
+                            out_ref[half, pl.ds(slab * 6 * CAP + at, 1), :] = block[halves - 1 - slab : halves - slab]
+
+
+def grid_kernel(local, senders, taps_ref, matrix_ref, twist_ref, out_ref, place_ref, grid_ref, high_ref, low_ref):
+    count = 2 * CAP * senders
+    for arr in range(3):
+        rows = 6 * CAP * local + arr * 2 * CAP
+        value = taps_ref[:, rows : rows + 2 * CAP, :].reshape(count, LANES)
+        place_ref[arr] = value.T
+    cell = lax.broadcasted_iota(jnp.int32, (TILE, count), 0).astype(F32)
+    wide = lax.broadcasted_iota(jnp.int32, (TILE, LANES), 1)
+    support = (HALF + 1.0) * (HALF + 1.0)
+
+    def bump(offset):
+        inner = jnp.maximum(support - offset * offset, 0.0)
+        return inner * inner
+
+    def column(j, carry):
+        sums = []
+        for row in range(2):
+            at = row * NT + j
+            tap_u = bump(cell - place_ref[1, pl.ds(at, 1), :])
+            tap_v = bump(cell - place_ref[2, pl.ds(at, 1), :]) * place_ref[0, pl.ds(at, 1), :]
+            u_high, u_low = split(tap_u)
+            v_high, v_low = split(tap_v)
+            product = lax.dot_general(
+                jnp.concatenate([v_high, v_low], axis=0),
+                jnp.concatenate([u_high, u_low], axis=0),
+                (((1,), (1,)), ((), ())),
+                preferred_element_type=F32,
+            )
+            value = product[:TILE] + product[TILE:]
+            sums.append(value + pltpu.roll(value, TILE, 1))
+        grid_ref[pl.ds(pl.multiple_of(j * TILE, TILE), TILE), :] = jnp.where(wide < TILE, sums[0], sums[1])
+        return carry
+
+    lax.fori_loop(0, NT, column, 0, unroll=2)
+    strip = 16
+
+    def transform(t, carry):
+        base = pl.multiple_of(t * strip, strip)
+        values = [grid_ref[pl.ds(pl.multiple_of(LANES * j + base, strip), strip), :] for j in range(COARSE)]
+        table = twist_ref[pl.ds(base, strip), :]
+        for q, (real, imag) in enumerate(real_transform(values)):
+            c = table[:, q : q + 1]
+            s = table[:, NT + q : NT + q + 1]
+            if imag is None:
+                turned = (real * c, real * s)
+            else:
+                turned = (real * c - imag * s, real * s + imag * c)
+            for part in range(2):
+                high, low = split(turned[part])
+                high_ref[q, pl.ds(part * LANES + base, strip), :] = high
+                low_ref[q, pl.ds(part * LANES + base, strip), :] = low
+        return carry
+
+    lax.fori_loop(0, LANES // strip, transform, 0)
+    peers, own = out_ref.shape[0], out_ref.shape[3]
+    for q in range(HERM):
+        high = high_ref[q]
+        value = jnp.dot(
+            matrix_ref[...], jnp.concatenate([high, low_ref[q], high], axis=0), preferred_element_type=F32
+        )
+        for peer in range(peers):
+            for part in range(2):
+                at = peer * 2 * own + part * own
+                out_ref[peer, part, q] = value[at : at + own]
+                if 0 < q < COARSE // 2:
+                    out_ref[peer, part, COARSE - q] = value[LANES + at : LANES + at + own]
+
+
+def image_kernel(first_ref, second_ref, matrix_ref, turn_ref, out_ref, high_ref, low_ref, stage_ref):
+    peers, own = first_ref.shape[0], first_ref.shape[3]
+    strip = 2 * own
+
+    def transform(t, carry):
+        values = [
+            tuple(ref[peer, part, pl.ds(2 * t, 2)].reshape(strip, LANES) for part in range(2))
+            for peer in range(peers)
+            for ref in (first_ref, second_ref)
+        ]
+        base = pl.multiple_of(t * strip, strip)
+        turned = [times(value, s / (2 * SLABS)) for s, value in enumerate(values)]
+        for odd, chosen in enumerate((values, turned)):
+            for k, (real, imag) in enumerate(complex_transform(chosen)):
+                q = 2 * k + odd
+                c, s = turn_ref[pl.ds(q, 1), :], turn_ref[pl.ds(COARSE + q, 1), :]
+                for part, value in enumerate((real * c - imag * s, real * s + imag * c)):
+                    high, low = split(value)
+                    high_ref[q, pl.ds(base, strip), part * LANES : (part + 1) * LANES] = high
+                    low_ref[q, pl.ds(base, strip), part * LANES : (part + 1) * LANES] = low
+        return carry
+
+    lax.fori_loop(0, COARSE // 2, transform, 0)
+    contract = (((1,), (1,)), ((), ()))
+    blocks = COARSE * own // LANES
+
+    def sums(q, carry):
+        both = lax.dot_general(matrix_ref[...], high_ref[q], contract, preferred_element_type=F32)
+        more = lax.dot_general(matrix_ref[:LANES], low_ref[q], contract, preferred_element_type=F32)
+        value = both[:LANES] + both[LANES:] + more
+        for block in range(blocks):
+            stage_ref[block, pl.ds(q, LANES, stride=COARSE), :] = value[:, block * LANES : (block + 1) * LANES]
+        return carry
+
+    lax.fori_loop(0, COARSE, sums, 0)
+    per = LANES // own
+
+    def turn(t, carry):
+        at = pl.multiple_of(t * LANES, LANES)
+        for block in range(blocks):
+            value = stage_ref[block, pl.ds(at, LANES), :].T
+            for k in range(per):
+                out_ref[:, block * per + k, pl.ds(at, LANES)] = value[k * own : (k + 1) * own]
+        return carry
+
+    lax.fori_loop(0, G // LANES, turn, 0)
+
+
+def constants(senders, own):
+    peers = LANES // HALVES // own
+    cell = np.arange(LANES, dtype=np.float64)
+    rows = []
+    for mirror in range(2):
+        for peer in range(peers):
+            p = peer * own + np.arange(own)
+            p = LANES - 1 - p if mirror else p
+            phase = 2 * np.pi * ((p[:, None] * cell[None, :]) % LANES) / LANES
+            sign = -1.0 if mirror else 1.0
+            rows.append(np.concatenate([np.cos(phase), -np.sin(phase)], axis=1))
+            rows.append(sign * np.concatenate([np.sin(phase), np.cos(phase)], axis=1))
+    high, low = split_constant(np.concatenate(rows, axis=0))
+    along_v = np.concatenate([high, high, low], axis=1)
+    phase = 2 * np.pi * ((np.arange(LANES)[:, None] * cell[None, :]) % LANES) / LANES
+    support = (HALF + 1.0) ** 8
+    scale = 1.0 / math.sqrt(senders * NT * NT * CAP) / support
+    high, low = split_constant(scale * np.concatenate([np.cos(phase), -np.sin(phase)], axis=1))
+    along_u = np.concatenate([high, low], axis=0)
+    q = np.arange(COARSE)
+    phase = 2 * np.pi * q[:, None] * cell[None, :] / G
+    turn = np.concatenate([np.cos(phase), np.sin(phase)], axis=0).astype(np.float32)
+    twist = np.zeros((LANES, 2 * NT))
+    twist[:, :HERM] = np.cos(phase[:HERM]).T
+    twist[:, NT : NT + HERM] = np.sin(phase[:HERM]).T
+    return along_v, along_u, turn, twist.astype(np.float32)
+
+
+def fast_body(sample_weight, fraction_u, fraction_v, cell_code, tile_fill):
+    group = ("half", "quarter", "chan")
+    inner = ("quarter", "chan")
+    senders = lax.axis_size(group)
+    peers = lax.axis_size(inner)
+    own = LANES // senders
+    along_v, along_u, turn, twist = constants(senders, own)
+    flip = 1.0 - 2.0 * (lax.axis_index("half") * (jnp.arange(LANES, dtype=jnp.int32) % 2)).astype(F32)
+    twist = twist * flip[:, None]
+    packed = pl.pallas_call(
+        pack_kernel,
+        out_shape=jax.ShapeDtypeStruct((HALVES, SLABS * 6 * CAP, LANES), F32),
+        scratch_shapes=[pltpu.VMEM((6, NT, LANES), F32)],
+        name="pack",
+    )(sample_weight, fraction_u, fraction_v, cell_code, tile_fill)
+    packed = packed.reshape(senders, SLABS * 6 * CAP * HALVES // senders, LANES)
+    taps = lax.all_to_all(packed, group, split_axis=0, concat_axis=0, tiled=True)
+    received = []
+    for local in range(SLABS // peers):
+        spectrum = pl.pallas_call(
+            lambda *refs, local=local: grid_kernel(local, senders, *refs),
+            out_shape=jax.ShapeDtypeStruct((peers, 2, COARSE, own, LANES), F32),
+            scratch_shapes=[
+                pltpu.VMEM((3, LANES, 2 * CAP * senders), F32),
+                pltpu.VMEM((COARSE * LANES, LANES), F32),
+                pltpu.VMEM((HERM, 2 * LANES, LANES), BF16),
+                pltpu.VMEM((HERM, 2 * LANES, LANES), BF16),
+            ],
+            name=f"grid_{local}",
+        )(taps, along_v, twist)
+        received.append(lax.all_to_all(spectrum, inner, split_axis=0, concat_axis=0, tiled=True))
+    image = pl.pallas_call(
+        image_kernel,
+        out_shape=jax.ShapeDtypeStruct((own, COARSE, G), F32),
+        scratch_shapes=[
+            pltpu.VMEM((COARSE, COARSE * own, 2 * LANES), BF16),
+            pltpu.VMEM((COARSE, COARSE * own, 2 * LANES), BF16),
+            pltpu.VMEM((COARSE * own // LANES, G, LANES), F32),
+        ],
+        name="image",
+    )(*received, along_u, turn)
+    return image.reshape(own * COARSE, G)
+
+
 def solution(mesh):
+    layouts, tiles, chans = (mesh.shape[name] for name in ("layout", "tile", "chan"))
+    if tiles % HALVES == 0 and SLABS == tiles * chans // HALVES * 2 and LANES == 8 * tiles * chans:
+        mesh = Mesh(
+            mesh.devices.reshape(layouts, HALVES, tiles // HALVES, chans), ("layout", "half", "quarter", "chan")
+        )
+        first, program = ("layout", "half", "quarter", "chan"), fast_body
+    else:
+        first, program = ("layout", "tile", "chan"), general_body
     return jax.shard_map(
-        body,
+        program,
         mesh=mesh,
-        in_specs=(
-            P(("layout", "tile", "chan"), None, None),
-            P(("layout", "tile", "chan"), None, None),
-            P(("layout", "tile", "chan"), None, None),
-            P(("layout", "tile", "chan"), None, None),
-            P(("layout", "tile", "chan"), None, None),
-        ),
-        out_specs=P(("layout", "tile", "chan"), None),
+        in_specs=(P(first, None, None),) * 5,
+        out_specs=P(first, None),
         check_vma=False,
     )

time: 448 us -> 125 us (0.28)
  the two profiles are of different devices: /device:TPU:13 before, /device:TPU:0 now
where the time goes in v1:
time: 125 us; the launch traced here: 124 us
  Pallas kernels  59.6 us (48%)
  blocking collectives  30.3 us (24%)
  waiting for transfers between devices  20.9 us (17%)
  starting transfers between devices  11 us (9%)
  other arithmetic  1.56 us (1%)
    pallas_call x2, Pallas kernels, fast_body(): pl.pallas_call(lambda *refs, local=local: grid_kernel(local, senders, *re...  30.7 us
    all_to_all x1, blocking collectives, fast_body(): lax.all_to_all(spectrum, inner, split_axis=0, concat_axis=0, tiled=True)  30.3 us
    pallas_call x1, Pallas kernels, fast_body(): pl.pallas_call(image_kernel, out_shape=jax.ShapeDtypeStruct((own, COARSE,...  26.2 us
    all_to_all x1, waiting for transfers between devices, fast_body(): lax.all_to_all(packed, group, split_axis=0, concat_axis=0, tiled=True)  10.6 us
    all_to_all x1, waiting for transfers between devices, fast_body(): lax.all_to_all(spectrum, inner, split_axis=0, concat_axis=0, tiled=True)  10.3 us
    all_to_all x1, starting transfers between devices, fast_body(): lax.all_to_all(packed, group, split_axis=0, concat_axis=0, tiled=True)  7.41 us
    all_to_all x1, starting transfers between devices, fast_body(): lax.all_to_all(spectrum, inner, split_axis=0, concat_axis=0, tiled=True)  3.6 us
    pallas_call x1, Pallas kernels, fast_body(): pl.pallas_call(pack_kernel, out_shape=jax.ShapeDtypeStruct((HALVES, SLABS...  2.67 us
  transfers between devices with their start and end apart: 2, of which 2 were waited for; matrix products, arithmetic and copies ran while one was open for 1% of the time, Pallas kernels for 12%

profile of v1, /device:TPU:0, one launch (start us, length us, event | category | flops | bytes accessed | tf_op | source)
XLA Modules:
  0.0 124.2 jit_solution(13997309826133712036)
XLA Ops:
  0.0 2.7 %pack.1 = f32[2,384,128]{2,1,0:T(8,128)} custom-call(f32[1,64,256]{2,1,0:T(8,128)} %weight_ref.1, f32[1,64,256]{2,1,0:T(8,128)} %frac_u_ref.1, f32[1,64,256]{2,1,0:T(8,128)} %frac_v_ref.1, s32[1,64,256]{2,1,0:T(8,128)} %code_ref.1, s32[1,64,64]{2,1,0:T(8,128)} %fill_ref.1), custom_call_target="tpu_custom_call" | custom-call | tf_op jit(solution)/shard_map/pack/pallas_call | solution.py:413
  2.7 7.4 %all-to-all-start = ((f32[16,48,128]{2,1,0:T(8,128)}), f32[16,48,128]{2,1,0:T(8,128)S(1)}, u32[]{:S(2)}, u32[]{:S(2)}) async-start(f32[16,48,128]{2,1,0:T(8,128)} %bitcast.2), calls=%async_computation | async-start | bytes 786432 | tf_op jit(solution)/shard_map/all_to_all | solution.py:420
  10.1 1.5 %broadcast_multiply_fusion.refs_2_ = f32[128,128]{1,0:T(8,128)} fusion(f32[128,128]{1,0:T(8,128)} %constant.34.clone, f32[128]{0:T(128)S(1)} %fusion.3), kind=kLoop, calls=%fused_computation | loop fusion | flops 16384 | bytes 131584 | tf_op jit(solution)/shard_map/mul | solution.py:412
  11.7 10.6 %all-to-all-done.refs_0_ = f32[16,48,128]{2,1,0:T(8,128)S(1)} async-done(((f32[16,48,128]{2,1,0:T(8,128)}), f32[16,48,128]{2,1,0:T(8,128)S(1)}, u32[]{:S(2)}, u32[]{:S(2)}) %all-to-all-start) | async-done | bytes 393248 | tf_op jit(solution)/shard_map/all_to_all | solution.py:420
  22.3 0.0 copy-start.1
  22.3 0.7 copy-done.1
  23.0 15.4 %grid_1.1 = f32[8,2,32,8,128]{4,3,2,1,0:T(8,128)} custom-call(f32[16,48,128]{2,1,0:T(8,128)} %copy-done.1, bf16[256,768]{1,0:T(8,128)(2,1)} %constant.35.clone.refs_1_, f32[128,128]{1,0:T(8,128)} %broadcast_multiply_fusion.refs_2_), custom_call_target="tpu_custom_call" | custom-call | tf_op jit(solution)/shard_map/grid_1/pallas_call | solution.py:423
  38.4 3.6 %all-to-all-start.2 = ((f32[8,2,32,8,128]{4,3,2,1,0:T(8,128)}), f32[8,2,32,8,128]{4,3,2,1,0:T(8,128)S(1)}, u32[]{:S(2)}, u32[]{:S(2)}) async-start(f32[8,2,32,8,128]{4,3,2,1,0:T(8,128)} %grid_1.1), calls=%async_computation.2 | async-start | bytes 4194304 | tf_op jit(solution)/shard_map/all_to_all | solution.py:434
  42.0 15.4 %grid_0.1 = f32[8,2,32,8,128]{4,3,2,1,0:T(8,128)} custom-call(f32[16,48,128]{2,1,0:T(8,128)} %copy-done.1, bf16[256,768]{1,0:T(8,128)(2,1)} %constant.35.clone.refs_1_, f32[128,128]{1,0:T(8,128)} %broadcast_multiply_fusion.refs_2_), custom_call_target="tpu_custom_call" | custom-call | tf_op jit(solution)/shard_map/grid_0/pallas_call | solution.py:423
  57.3 10.3 %all-to-all-done.2.second_ref = f32[8,2,32,8,128]{4,3,2,1,0:T(8,128)S(1)} async-done(((f32[8,2,32,8,128]{4,3,2,1,0:T(8,128)}), f32[8,2,32,8,128]{4,3,2,1,0:T(8,128)S(1)}, u32[]{:S(2)}, u32[]{:S(2)}) %all-to-all-start.2) | async-done | bytes 2097184 | tf_op jit(solution)/shard_map/all_to_all | solution.py:434
  67.6 0.0 copy-start
  67.6 30.3 %all_to_all.15.first_ref = f32[8,2,32,8,128]{4,3,2,1,0:T(8,128)} all-to-all(f32[8,2,32,8,128]{4,3,2,1,0:T(8,128)} %grid_0.1), channel_id=1, replica_groups=mesh['layout'=2,'half'=2,'quarter'=4,'chan'=2] {'quarter','chan'}, dimensions={0} | all-to-all | bytes 4194304 | tf_op jit(solution)/shard_map/all_to_all | solution.py:434
  97.9 0.0 copy-done
  98.0 26.2 %image.1 = f32[8,32,4096]{2,1,0:T(8,128)} custom-call(f32[8,2,32,8,128]{4,3,2,1,0:T(8,128)} %all_to_all.15.first_ref, f32[8,2,32,8,128]{4,3,2,1,0:T(8,128)} %copy-done, bf16[256,256]{1,0:T(8,128)(2,1)} %constant.36.clone.matrix_ref, f32[64,128]{1,0:T(8,128)} %constant.37.clone.turn_ref), custom_call_target="tpu_custom_call" | custom-call | tf_op jit(solution)/shard_map/image/pallas_call | solution.py:435
  (1 shorter events, 0.0 us)
Async XLA Ops:
  2.7 19.6 %all-to-all-start = ((f32[16,48,128]{2,1,0:T(8,128)}), f32[16,48,128]{2,1,0:T(8,128)S(1)}, u32[]{:S(2)}, u32[]{:S(2)}) async-start(f32[16,48,128]{2,1,0:T(8,128)} %bitcast.2), calls=%async_computation | async-start | bytes 786432 | tf_op jit(solution)/shard_map/all_to_all | solution.py:420
  22.3 0.7 copy-start.1
  38.4 29.2 %all-to-all-start.2 = ((f32[8,2,32,8,128]{4,3,2,1,0:T(8,128)}), f32[8,2,32,8,128]{4,3,2,1,0:T(8,128)S(1)}, u32[]{:S(2)}, u32[]{:S(2)}) async-start(f32[8,2,32,8,128]{4,3,2,1,0:T(8,128)} %grid_1.1), calls=%async_computation.2 | async-start | bytes 4194304 | tf_op jit(solution)/shard_map/all_to_all | solution.py:434
  67.6 30.3 %copy-start = (f32[8,2,32,8,128]{4,3,2,1,0:T(8,128)}, f32[8,2,32,8,128]{4,3,2,1,0:T(8,128)S(1)}, u32[]{:S(2)}) copy-start(f32[8,2,32,8,128]{4,3,2,1,0:T(8,128)S(1)} %all-to-all-done.2.second_ref) | copy-start | bytes 6291460
